TPU v7x, 8 devices: a whole 2x2x1 slice. The times are simulated.
8 devices in a mesh: side: 4 (over z, y, x), rep: 2 (over core).
Axes of the slice: x: 2, y: 2, z: 1, core: 2. Of those that a mesh axis runs over, the one named last changes fastest.
Arguments:
- w_up: float32 [4, 12, 960, 1280], P('side', None, 'rep')
- w_down: float32 [4, 12, 1280, 960], P('side', None, None, 'rep')
- g_up: float32 [4, 12, 960, 1280], P('side', None, 'rep')
- g_down: float32 [4, 12, 1280, 960], P('side', None, None, 'rep')
- learn_rate: float32 [], replicated
- prompts: bfloat16 [4, 8192, 480], P('side', 'rep')
- prompt_lens: int32 [2], P('rep')
Outputs:
- output 1: float32 [4, 12, 960, 1280], P('side', None, 'rep')
- output 2: float32 [4, 12, 1280, 960], P('side', None, None, 'rep')
- output 3: bfloat16 [4, 8192, 480], P('side', 'rep')
All inputs are finite; a program needn't handle non-finite values.
Results may differ from a plain program's by a relative error of at most 0.02.
Values are sent between devices in bfloat16 or wider.
A program may use at most 1 GiB of HBM per device.

v0:
```python
import jax
import jax.numpy as jnp
from jax import lax
from jax.sharding import PartitionSpec as P


def solution(mesh):
    side_devs = mesh.shape["side"]
    tp_ways = side_devs // 2
    cross_perm = [(src_pos, src_pos + tp_ways) for src_pos in range(tp_ways)]
    up_spec = P("side", None, "rep", None)
    down_spec = P("side", None, None, "rep")
    act_spec = P("side", "rep", None)

    def device_step(w_up, w_down, g_up, g_down, learn_rate, prompts, prompt_lens):
        new_up = w_up - learn_rate * g_up
        new_down = w_down - learn_rate * g_down
        up_sent = lax.ppermute(new_up[0].astype(jnp.bfloat16), "side", cross_perm)
        down_sent = lax.ppermute(new_down[0].astype(jnp.bfloat16), "side", cross_perm)
        up_full = lax.all_gather(up_sent, "rep", axis=1, tiled=True)
        down_full = lax.all_gather(down_sent, "rep", axis=2, tiled=True)
        side_idx = lax.axis_index("side")
        is_gen = side_idx >= tp_ways
        tokens = prompts.shape[1]
        d_piece = prompts.shape[2]
        if tp_ways > 1:
            pieces = lax.all_gather(prompts[0], "side", axis=0)
            hidden = jnp.transpose(pieces[tp_ways:], (1, 0, 2)).reshape(tokens, tp_ways * d_piece)
        else:
            hidden = prompts[0]
        for layer_idx in range(up_full.shape[0]):
            pre_act = jnp.dot(hidden, up_full[layer_idx], preferred_element_type=jnp.float32)
            act_bf = jax.nn.gelu(pre_act, approximate=True).astype(jnp.bfloat16)
            part_sum = jnp.dot(act_bf, down_full[layer_idx], preferred_element_type=jnp.float32)
            if tp_ways > 1:
                part_sum = lax.psum(jnp.where(is_gen, part_sum, 0.0), "side")
            hidden = (hidden.astype(jnp.float32) + part_sum).astype(jnp.bfloat16)
        keep_mask = jnp.arange(tokens)[:, None] < prompt_lens[0]
        tp_idx = jnp.maximum(side_idx - tp_ways, 0)
        own_cols = lax.dynamic_slice_in_dim(hidden, tp_idx * d_piece, d_piece, axis=1)
        out_block = jnp.where(keep_mask & is_gen, own_cols, jnp.zeros_like(own_cols))
        return new_up, new_down, out_block[None]

    mapped = jax.shard_map(
        device_step,
        mesh=mesh,
        in_specs=(up_spec, down_spec, up_spec, down_spec, P(), act_spec, P("rep")),
        out_specs=(up_spec, down_spec, act_spec),
        check_vma=False,
    )
    return mapped
```

profile of v0, /device:TPU:0, one launch (start us, length us, event | category | flops | bytes accessed | tf_op | source)
XLA Modules:
  0.0 4678.6 jit_solution(10087520526954614655)
XLA Ops:
  7.2 0.7 all-gather.4.cloned.1.call-update
  8.6 33.9 convert_bitcast_fusion.1
  42.5 10.5 collective-permute-start
  53.0 411.7 %collective-permute-done = bf16[12,480,1280]{2,1,0:T(8,128)(2,1)} collective-permute-done((bf16[12,480,1280]{2,1,0:T(8,128)(2,1)}, bf16[12,480,1280]{2,1,0:T(8,128)(2,1)}, u32[]{:S(2)}, u32[]{:S(2)}) %collective-permute-start) | collective-permute-done | bytes 14745632 | tf_op jit(solution)/shard_map/ppermute | solution.py:18
  464.7 33.9 convert_bitcast_fusion
  498.7 9.6 collective-permute-start.1
  508.3 310.7 %collective-permute-done.1 = bf16[12,1280,480]{1,2,0:T(8,128)(2,1)} collective-permute-done((bf16[12,1280,480]{1,2,0:T(8,128)(2,1)}, bf16[12,1280,480]{1,2,0:T(8,128)(2,1)}, u32[]{:S(2)}, u32[]{:S(2)}) %collective-permute-start.1) | collective-permute-done | bytes 14745632 | tf_op jit(solution)/shard_map/ppermute | solution.py:19
  819.1 7.5 slice.100
  826.6 37.7 all-gather.8.cloned.1.call-done
  864.3 29.2 convolution_select_fusion.11
  893.5 12.0 all-reduce.15.cloned.1.call-start
  905.5 268.1 %all-reduce.13.cloned.1.call-done = f32[4096,960]{0,1:T(8,128)} async-done(((f32[4096,960]{0,1:T(8,128)}), f32[4096,960]{0,1:T(8,128)}) %all-reduce.13.cloned.1.call-update) | async-done | bytes 15728656 | tf_op jit(solution)/shard_map/psum | solution.py:36
  1173.6 11.2 add_convert_fusion.10
  1184.9 29.4 convolution_select_fusion.10
  1214.3 278.9 %all-reduce.15.cloned.1.call-done = f32[4096,960]{0,1:T(8,128)} async-done(((f32[4096,960]{0,1:T(8,128)}), f32[4096,960]{0,1:T(8,128)}) %all-reduce.15.cloned.1.call-update) | async-done | bytes 15728656 | tf_op jit(solution)/shard_map/psum | solution.py:36
  1493.2 30.3 convolution_select_fusion.9
  1523.5 0.4 all-reduce.19.cloned.1.call-start
  1524.0 278.5 %all-reduce.17.cloned.1.call-done = f32[4096,960]{0,1:T(8,128)} async-done(((f32[4096,960]{0,1:T(8,128)}), f32[4096,960]{0,1:T(8,128)}) %all-reduce.17.cloned.1.call-update) | async-done | bytes 15728656 | tf_op jit(solution)/shard_map/psum | solution.py:36
  1802.5 16.6 add_convert_fusion.8
  1819.1 29.4 convolution_select_fusion.8
  1848.5 0.2 all-reduce.21.cloned.1.call-start
  1848.7 278.7 %all-reduce.19.cloned.1.call-done = f32[4096,960]{0,1:T(8,128)} async-done(((f32[4096,960]{0,1:T(8,128)}), f32[4096,960]{0,1:T(8,128)}) %all-reduce.19.cloned.1.call-update) | async-done | bytes 15728656 | tf_op jit(solution)/shard_map/psum | solution.py:36
  2127.4 30.3 convolution_select_fusion.7
  2157.8 278.9 %all-reduce.21.cloned.1.call-done = f32[4096,960]{0,1:T(8,128)} async-done(((f32[4096,960]{0,1:T(8,128)}), f32[4096,960]{0,1:T(8,128)}) %all-reduce.21.cloned.1.call-update) | async-done | bytes 15728656 | tf_op jit(solution)/shard_map/psum | solution.py:36
  2436.7 16.6 add_convert_fusion.6
  2453.2 29.4 convolution_select_fusion.6
  2482.7 0.4 all-reduce.25.cloned.1.call-start
  2483.1 278.5 %all-reduce.23.cloned.1.call-done = f32[4096,960]{0,1:T(8,128)} async-done(((f32[4096,960]{0,1:T(8,128)}), f32[4096,960]{0,1:T(8,128)}) %all-reduce.23.cloned.1.call-update) | async-done | bytes 15728656 | tf_op jit(solution)/shard_map/psum | solution.py:36
  2761.6 30.3 convolution_select_fusion.5
  2791.9 0.0 all-reduce.27.cloned.1.call-start
  2792.0 278.9 %all-reduce.25.cloned.1.call-done = f32[4096,960]{0,1:T(8,128)} async-done(((f32[4096,960]{0,1:T(8,128)}), f32[4096,960]{0,1:T(8,128)}) %all-reduce.25.cloned.1.call-update) | async-done | bytes 15728656 | tf_op jit(solution)/shard_map/psum | solution.py:36
  3070.9 16.6 add_convert_fusion.4
  3087.5 29.4 convolution_select_fusion.4
  3116.9 0.2 all-reduce.29.cloned.1.call-start
  3117.1 278.7 %all-reduce.27.cloned.1.call-done = f32[4096,960]{0,1:T(8,128)} async-done(((f32[4096,960]{0,1:T(8,128)}), f32[4096,960]{0,1:T(8,128)}) %all-reduce.27.cloned.1.call-update) | async-done | bytes 15728656 | tf_op jit(solution)/shard_map/psum | solution.py:36
  3395.8 30.3 convolution_select_fusion.3
  3426.2 278.9 %all-reduce.29.cloned.1.call-done = f32[4096,960]{0,1:T(8,128)} async-done(((f32[4096,960]{0,1:T(8,128)}), f32[4096,960]{0,1:T(8,128)}) %all-reduce.29.cloned.1.call-update) | async-done | bytes 15728656 | tf_op jit(solution)/shard_map/psum | solution.py:36
  3705.1 16.6 add_convert_fusion.2
  3721.7 29.4 convolution_select_fusion.2
  3751.1 0.4 all-reduce.33.cloned.1.call-start
  3751.5 278.5 %all-reduce.31.cloned.1.call-done = f32[4096,960]{0,1:T(8,128)} async-done(((f32[4096,960]{0,1:T(8,128)}), f32[4096,960]{0,1:T(8,128)}) %all-reduce.31.cloned.1.call-update) | async-done | bytes 15728656 | tf_op jit(solution)/shard_map/psum | solution.py:36
  4030.0 30.3 convolution_select_fusion.1
  4060.3 0.2 all-reduce.35.cloned.1.call-start
  4060.5 278.7 %all-reduce.33.cloned.1.call-done = f32[4096,960]{0,1:T(8,128)} async-done(((f32[4096,960]{0,1:T(8,128)}), f32[4096,960]{0,1:T(8,128)}) %all-reduce.33.cloned.1.call-update) | async-done | bytes 15728656 | tf_op jit(solution)/shard_map/psum | solution.py:36
  4339.3 16.6 add_convert_fusion
  4355.9 29.4 convolution_select_fusion
  4385.9 278.3 %all-reduce.35.cloned.1.call-done = f32[4096,960]{0,1:T(8,128)} async-done(((f32[4096,960]{0,1:T(8,128)}), f32[4096,960]{0,1:T(8,128)}) %all-reduce.35.cloned.1.call-update) | async-done | bytes 15728656 | tf_op jit(solution)/shard_map/psum | solution.py:36
  4664.2 7.7 fusion.98
  (24 shorter events, 0.5 us)
Async XLA Ops:
  7.2 811.9 %all-gather.4.cloned.1.call-start = ((), (), s32[]{:S(2)}) async-start(), calls=%async_computation | async-start | bytes 19660800 | tf_op jit(solution)/shard_map/all_gather | solution.py:27
  7.9 818.7 %all-gather.6.cloned.1.call-start = ((), (), s32[]{:S(2)}) async-start(), calls=%async_computation.1 | async-start | bytes 44236800 | tf_op jit(solution)/shard_map/all_gather | solution.py:20
  42.5 422.2 %collective-permute-start = (bf16[12,480,1280]{2,1,0:T(8,128)(2,1)}, bf16[12,480,1280]{2,1,0:T(8,128)(2,1)}, u32[]{:S(2)}, u32[]{:S(2)}) collective-permute-start(bf16[12,480,1280]{2,1,0:T(8,128)(2,1)} %get-tuple-element.5), channel_id=1, source_target_pairs={{0,4},{2,6},{1,5},{3,7}} | collective-permute-start | bytes 44236808 | tf_op jit(solution)/shard_map/ppermute | solution.py:18
  464.7 399.6 %all-gather.8.cloned.1.call-start = ((), (), s32[]{:S(2)}) async-start(), calls=%async_computation.2 | async-start | bytes 44236800 | tf_op jit(solution)/shard_map/all_gather | solution.py:21
  498.7 320.3 %collective-permute-start.1 = (bf16[12,1280,480]{1,2,0:T(8,128)(2,1)}, bf16[12,1280,480]{1,2,0:T(8,128)(2,1)}, u32[]{:S(2)}, u32[]{:S(2)}) collective-permute-start(bf16[12,1280,480]{1,2,0:T(8,128)(2,1)} %get-tuple-element.3), channel_id=1, source_target_pairs={{0,4},{2,6},{1,5},{3,7}} | collective-permute-start | bytes 44236808 | tf_op jit(solution)/shard_map/ppermute | solution.py:19
  819.0 354.6 %all-reduce.13.cloned.1.call-start = ((), (), s32[]{:S(2)}) async-start(), calls=%async_computation.3 | async-start | bytes 31457280 | tf_op jit(solution)/shard_map/psum | solution.py:36
  893.5 599.7 %all-reduce.15.cloned.1.call-start = ((), (), s32[]{:S(2)}) async-start(), calls=%async_computation.4 | async-start | bytes 31457280 | tf_op jit(solution)/shard_map/psum | solution.py:36
  1214.3 588.2 %all-reduce.17.cloned.1.call-start = ((), (), s32[]{:S(2)}) async-start(), calls=%async_computation.5 | async-start | bytes 31457280 | tf_op jit(solution)/shard_map/psum | solution.py:36
  1523.5 603.9 %all-reduce.19.cloned.1.call-start = ((), (), s32[]{:S(2)}) async-start(), calls=%async_computation.6 | async-start | bytes 31457280 | tf_op jit(solution)/shard_map/psum | solution.py:36
  1848.5 588.2 %all-reduce.21.cloned.1.call-start = ((), (), s32[]{:S(2)}) async-start(), calls=%async_computation.7 | async-start | bytes 31457280 | tf_op jit(solution)/shard_map/psum | solution.py:36
  2157.7 603.9 %all-reduce.23.cloned.1.call-start = ((), (), s32[]{:S(2)}) async-start(), calls=%async_computation.8 | async-start | bytes 31457280 | tf_op jit(solution)/shard_map/psum | solution.py:36
  2482.7 588.2 %all-reduce.25.cloned.1.call-start = ((), (), s32[]{:S(2)}) async-start(), calls=%async_computation.9 | async-start | bytes 31457280 | tf_op jit(solution)/shard_map/psum | solution.py:36
  2791.9 603.9 %all-reduce.27.cloned.1.call-start = ((), (), s32[]{:S(2)}) async-start(), calls=%async_computation.10 | async-start | bytes 31457280 | tf_op jit(solution)/shard_map/psum | solution.py:36
  3116.9 588.2 %all-reduce.29.cloned.1.call-start = ((), (), s32[]{:S(2)}) async-start(), calls=%async_computation.11 | async-start | bytes 31457280 | tf_op jit(solution)/shard_map/psum | solution.py:36
  3426.1 603.9 %all-reduce.31.cloned.1.call-start = ((), (), s32[]{:S(2)}) async-start(), calls=%async_computation.12 | async-start | bytes 31457280 | tf_op jit(solution)/shard_map/psum | solution.py:36
  3751.1 588.2 %all-reduce.33.cloned.1.call-start = ((), (), s32[]{:S(2)}) async-start(), calls=%async_computation.13 | async-start | bytes 31457280 | tf_op jit(solution)/shard_map/psum | solution.py:36
  4060.3 603.9 %all-reduce.35.cloned.1.call-start = ((), (), s32[]{:S(2)}) async-start(), calls=%async_computation.14 | async-start | bytes 31457280 | tf_op jit(solution)/shard_map/psum | solution.py:36
Sparse Core Ops, SparseCore 0:
  9.7 245.1 all-gather.3
  464.8 45.0 all-gather.5
  819.1 45.0 all-gather.7
  893.6 279.9 all-reduce.12
  1214.4 278.7 all-reduce.14
  1523.6 278.7 all-reduce.16
  1848.6 278.7 all-reduce.18
  2157.8 278.7 all-reduce.20
  2482.8 278.8 all-reduce.22
  2792.0 278.7 all-reduce.24
  3117.0 278.7 all-reduce.26
  3426.2 278.7 all-reduce.28
  3751.2 278.8 all-reduce.30
  4060.4 278.7 all-reduce.32
  4385.4 278.8 all-reduce.34
where the time goes:
time: 4690 us; the launch traced here: 4680 us
  waiting for transfers between devices  4090 us (87%)
  matrix products  357 us (8%)
  other arithmetic  170 us (4%)
    psum x12, waiting for transfers between devices, device_step(): part_sum = lax.psum(jnp.where(is_gen, part_sum, 0.0), 'side')  3330 us
    ppermute x1, waiting for transfers between devices, device_step(): up_sent = lax.ppermute(new_up[0].astype(jnp.bfloat16), 'side', cross_perm)  412 us
    dot_general x12, matrix products, device_step(): jnp.dot(act_bf, down_full[layer_idx], preferred_element_type=jnp.float32)  357 us
    ppermute x1, waiting for transfers between devices, device_step(): lax.ppermute(new_down[0].astype(jnp.bfloat16), 'side', cross_perm)  311 us
    convert_element_type x6, other arithmetic, device_step(): hidden = (hidden.astype(jnp.float32) + part_sum).astype(jnp.bfloat16)  94.2 us
  transfers between devices with their start and end apart: 17, of which 15 were waited for; matrix products, arithmetic and copies ran while one was open for 2% of the time, Pallas kernels for 0%

commit v1 on v0

v1 whole, which is shorter than its diff:
```python
import jax
import jax.numpy as jnp
from jax import lax
from jax.experimental import pallas as pl
from jax.experimental.pallas import tpu as pltpu
from jax.sharding import PartitionSpec as P


LATE_SHARE = 1
DIRECT_DOWN = 2
TILE = 256
ROW_RUN = 128
CHUNKS = (256, 256, 256, 256, 256)
LAST = (((1,), (1,)), ((), ()))
GELU_A = 0.7978845608
GELU_B = 0.7978845608 * 0.044715


def update_kernel(gen_ref, lr_ref, wu, gu, wd, gd, *refs):
    nu, nd, ub, db = refs[-4:]
    is_gen = gen_ref[0] == 1
    lr = lr_ref[0]

    @pl.when(is_gen)
    def _():
        nu[...] = jnp.zeros_like(nu)
        nd[...] = jnp.zeros_like(nd)

    @pl.when(jnp.logical_not(is_gen))
    def _():
        u = wu[...] - lr * gu[...]
        nu[...] = u
        ub[...] = u[0].astype(jnp.bfloat16)
        d = wd[...] - lr * gd[...]
        nd[...] = d
        db[...] = d[0].astype(jnp.bfloat16)


def update_group(gen, lr, w_up, g_up, w_down, g_down, prev, first, count):
    _, _, du, hp = w_up.shape
    split = 2
    ur = du // split

    def in_map(l, s, gen_ref, lr_ref):
        live = 1 - gen_ref[0]
        return (0, (first + l) * live, s * live, 0)

    def out_map(l, s, gen_ref, lr_ref):
        return (0, first + l, s, 0)

    def bf_map(l, s, gen_ref, lr_ref):
        return (l, s, 0)

    in_specs = [
        pl.BlockSpec((1, 1, ur, hp), in_map),
        pl.BlockSpec((1, 1, ur, hp), in_map),
        pl.BlockSpec((1, 1, ur, hp), in_map),
        pl.BlockSpec((1, 1, ur, hp), in_map),
    ]
    args = [w_up, g_up, w_down, g_down]
    aliases = {}
    if prev is not None:
        in_specs += [pl.BlockSpec(memory_space=pl.ANY)] * 2
        args += list(prev)
        aliases = {6: 0, 7: 1}
    nbytes = count * 2 * du * hp * 14
    return pl.pallas_call(
        update_kernel,
        grid_spec=pltpu.PrefetchScalarGridSpec(
            num_scalar_prefetch=2,
            grid=(count, split),
            in_specs=in_specs,
            out_specs=[
                pl.BlockSpec((1, 1, ur, hp), out_map),
                pl.BlockSpec((1, 1, ur, hp), out_map),
                pl.BlockSpec((1, ur, hp), bf_map),
                pl.BlockSpec((1, ur, hp), bf_map),
            ],
        ),
        out_shape=[
            jax.ShapeDtypeStruct(w_up.shape, jnp.float32),
            jax.ShapeDtypeStruct(w_down.shape, jnp.float32),
            jax.ShapeDtypeStruct((count, du, hp), jnp.bfloat16),
            jax.ShapeDtypeStruct((count, du, hp), jnp.bfloat16),
        ],
        input_output_aliases=aliases,
        cost_estimate=pl.CostEstimate(flops=nbytes * 30, bytes_accessed=nbytes, transcendentals=0),
        name="update",
    )(gen, lr, *args)


def gelu(z):
    t = jnp.tanh(z * (GELU_A + GELU_B * (z * z)))
    h = 0.5 * z
    return h + h * t


def mlp_kernel(live_ref, x_ref, *refs):
    ups, downs, out = refs[0:4], refs[4:8], refs[8]

    @pl.when(live_ref[pl.program_id(0)] == 1)
    def _():
        x0, x1 = x_ref[0], x_ref[1]
        acc0 = acc1 = None
        for q in range(2):
            at = 0
            for width in CHUNKS:
                cols = pl.ds(at, width)
                z = jnp.dot(x0, ups[2 * q][0, :, cols], preferred_element_type=jnp.float32)
                z = z + jnp.dot(x1, ups[2 * q + 1][0, :, cols], preferred_element_type=jnp.float32)
                u = gelu(z).astype(jnp.bfloat16)
                p0 = lax.dot_general(u, downs[2 * q][0, :, cols], LAST, preferred_element_type=jnp.float32)
                p1 = lax.dot_general(u, downs[2 * q + 1][0, :, cols], LAST, preferred_element_type=jnp.float32)
                acc0 = p0 if acc0 is None else acc0 + p0
                acc1 = p1 if acc1 is None else acc1 + p1
                at += width
        out[0] = (x0.astype(jnp.float32) + acc0).astype(jnp.bfloat16)
        out[1] = (x1.astype(jnp.float32) + acc1).astype(jnp.bfloat16)


def mlp_layer(live, act, ups, downs):
    _, rows, half = act.shape
    hp = ups[0][0].shape[2]

    def weight_spec(shape, place):
        return pl.BlockSpec((1,) + shape, lambda i, live_ref: (place, 0, 0), pipeline_mode=pl.Buffered(1))

    specs = [pl.BlockSpec((2, TILE, half), lambda i, live_ref: (0, i, 0))]
    specs += [weight_spec((half, hp), place) for _, place in ups]
    specs += [weight_spec((half, hp), place) for _, place in downs]
    flops = rows * 2 * half * 2 * hp * 4
    return pl.pallas_call(
        mlp_kernel,
        grid_spec=pltpu.PrefetchScalarGridSpec(
            num_scalar_prefetch=1,
            grid=(rows // TILE,),
            in_specs=specs,
            out_specs=pl.BlockSpec((2, TILE, half), lambda i, live_ref: (0, i, 0)),
        ),
        out_shape=jax.ShapeDtypeStruct(act.shape, jnp.bfloat16),
        compiler_params=pltpu.CompilerParams(vmem_limit_bytes=56 * 1024 * 1024),
        cost_estimate=pl.CostEstimate(flops=flops, bytes_accessed=24 * 1024 * 1024, transcendentals=rows * 2 * hp),
    )(live, act, *[a for a, _ in ups], *[a for a, _ in downs])


def solution(mesh):
    reps = mesh.shape["rep"]
    axes = ("side", "rep")

    def at(side, rep):
        return side * reps + rep

    pairs = [(t, c) for t in range(2) for c in range(2)]
    trade = [(at(t, c), at(1 - t, c)) for t, c in pairs]
    to_gen = [(at(t, c), at(2 + t, c)) for t, c in pairs]
    gen_trade = [(at(2 + t, c), at(3 - t, c)) for t, c in pairs]
    to_train = [(at(2 + t, c), at(t, c)) for t, c in pairs]
    core_swap = [(at(t, c), at(t, 1 - c)) for t, c in pairs]

    up_spec = P("side", None, "rep", None)
    down_spec = P("side", None, None, "rep")
    act_spec = P("side", "rep", None)

    def device_step(w_up, w_down, g_up, g_down, learn_rate, prompts, prompt_lens):
        side = lax.axis_index("side")
        core = lax.axis_index("rep")
        is_gen = side >= 2
        t = lax.rem(side, 2)
        tokens, half = prompts.shape[1], prompts.shape[2]
        part = tokens // 4

        gen = is_gen.astype(jnp.int32).reshape(1)
        lr = learn_rate.reshape(1)
        other_len = lax.ppermute(prompt_lens, "rep", [(0, 1), (1, 0)])

        def send(x, pairs):
            return lax.ppermute(x, axes, pairs)

        def after(x, *gates):
            gates = [g for g in gates if g is not None]
            return lax.optimization_barrier((x, *gates))[0] if gates else x

        w_down, g_down = jnp.swapaxes(w_down, 2, 3), jnp.swapaxes(g_down, 2, 3)
        layers = w_up.shape[1]

        prev = None
        own = []
        for layer in range(layers):
            new_up, new_down, ub, db = update_group(gen, lr, w_up, g_up, w_down, g_down, prev, layer, 1)
            prev = (new_up, new_down)
            own.append((ub, db))

        runs = jnp.swapaxes(prompts[0], 0, 1).reshape(half, part // ROW_RUN, 4, ROW_RUN)
        got = {}
        for dt in range(2):
            for dc in range(2):
                j = 2 * jnp.bitwise_xor(t, dt) + jnp.bitwise_xor(core, dc)
                mine = lax.dynamic_slice_in_dim(runs, j, 1, axis=2).reshape(half, part)
                perm = [(at(2 + a, b), at(a ^ dt, b ^ dc)) for a, b in pairs]
                got[dt, dc] = send(mine, perm)

        first = []
        for layer, (ub, db) in enumerate(own):
            ru = send(ub, trade)
            rd = send(db, trade if layer < DIRECT_DOWN else to_gen)
            first.append((ru, rd))
        own_p = [(send(ub, core_swap), send(db, core_swap)) for ub, db in own]

        swap = jnp.bitwise_xor(t, core) == 1
        near = jnp.concatenate([got[0, 0], got[0, 1]], axis=1)
        far = jnp.concatenate([got[1, 0], got[1, 1]], axis=1)
        act = jnp.swapaxes(jnp.stack([jnp.where(swap, far, near), jnp.where(swap, near, far)]), 1, 2)

        tiles = part // TILE
        first_row = jnp.arange(tiles) * (4 * TILE) + (2 * t + core) * ROW_RUN
        live = jnp.concatenate([first_row < prompt_lens[0], first_row < other_len[0]])
        live = (live & jnp.logical_not(is_gen)).astype(jnp.int32)

        second, last, recv, recv_p = {}, {}, {}, {}

        def second_hop(layer, act):
            if DIRECT_DOWN <= layer < layers:
                second[layer] = send(after(first[layer][1], act), gen_trade)

        def last_hop(layer, act):
            if DIRECT_DOWN <= layer < layers:
                last[layer] = send(after(second[layer], act), to_train)

        def share(layer, act):
            if layer >= layers:
                return
            ru, rd = first[layer]
            if layer >= DIRECT_DOWN:
                rd = last[layer]
            hops = (second.get(layer + 1), first[layer + 2][1] if layer + 2 < layers else None)
            ru, rd = after(ru, act), after(rd, act, *hops)
            recv[layer] = (ru, rd)
            recv_p[layer] = (send(ru, core_swap), send(rd, core_swap))

        for layer in range(layers):
            if layer == 0:
                for early in range(3):
                    second_hop(early, None)
                for early in range(2):
                    last_hop(early, None)
                share(0, None)
            gate = act if layer else None
            second_hop(layer + 3, gate)
            last_hop(layer + 2, gate)
            if layer + 1 < layers - LATE_SHARE:
                share(layer + 1, gate)
            elif layer not in recv:
                share(layer, gate)
            ups = [(w[layer][0], 0) for w in (own, own_p, recv, recv_p)]
            downs = [(w[layer][1], 0) for w in (own, own_p, recv, recv_p)]
            act = mlp_layer(live, act, ups, downs)

        act = jnp.swapaxes(act, 1, 2)
        back = {}
        for dt in range(2):
            halves = (act[0], act[1]) if dt == 0 else (act[1], act[0])
            cols = jnp.where(swap, halves[1], halves[0])
            for dc in range(2):
                perm = [(at(a, b), at(2 + (a ^ dt), b ^ dc)) for a, b in pairs]
                back[dt, dc] = lax.ppermute(cols[:, dc * part : (dc + 1) * part], axes, perm)
        by_core = {}
        for dt in range(2):
            lo, hi = back[dt, 0], back[dt, 1]
            by_core[dt] = [jnp.where(core == 0, lo, hi), jnp.where(core == 0, hi, lo)]
        ordered = [jnp.where(t == 0, by_core[0][c], by_core[1][c]) for c in range(2)]
        ordered += [jnp.where(t == 0, by_core[1][c], by_core[0][c]) for c in range(2)]
        y = jnp.stack([o.reshape(half, part // ROW_RUN, ROW_RUN) for o in ordered], axis=2)
        y = y.reshape(half, tokens)
        keep = (jnp.arange(tokens)[None, :] < prompt_lens[0]) & is_gen
        y = jnp.swapaxes(jnp.where(keep, y, jnp.zeros_like(y)), 0, 1)
        return prev[0], jnp.swapaxes(prev[1], 2, 3), y[None]

    return jax.shard_map(
        device_step,
        mesh=mesh,
        in_specs=(up_spec, down_spec, up_spec, down_spec, P(), act_spec, P("rep")),
        out_specs=(up_spec, down_spec, act_spec),
        check_vma=False,
    )
```

time: 4690 us -> 1140 us (0.24)
  waiting for transfers between devices: 4090 us -> 200 us
  Pallas kernels: 0 us -> 611 us
  matrix products: 357 us -> 0 us
  starting transfers between devices: 34.4 us -> 218 us
  other arithmetic: 170 us -> 14.9 us
  local copies, waits for them, and re-layouts: 7.47 us -> 76.6 us
    psum x12 -> x0, waiting for transfers between devices: 3330 us -> none  [device_step(): part_sum = lax.psum(jnp.where(is_gen, part_sum, 0.0), 'side')]
    pallas_call x0 -> x24, Pallas kernels: none -> 611 us  [the longest x12 534 us: mlp_layer(): pl.pallas_call(mlp_kernel, grid_spec=pltpu.PrefetchScalarGridSpec(num_sca...]
    ppermute x2 -> x101, waiting for transfers between devices: 722 us -> 200 us  [the longest x96 124 us: send(): return lax.ppermute(x, axes, pairs)]
    dot_general x12 -> x0, matrix products: 357 us -> none  [device_step(): jnp.dot(act_bf, down_full[layer_idx], preferred_element_type=jnp.float32)]
    ppermute x2 -> x101, starting transfers between devices: 20.1 us -> 218 us  [the longest x96 212 us: send(): return lax.ppermute(x, axes, pairs)]
    convert_element_type x8 -> x1, other arithmetic: 162 us -> 0.67 us  [device_step(): live = (live & jnp.logical_not(is_gen)).astype(jnp.int32)]
  transfers between devices with their start and end apart: 17 -> 101, of which waited for: 15 -> 16; matrix products, arithmetic and copies ran while one was open for 2% -> 2% of each run, Pallas kernels for 0% -> 50%
where the time goes in v1:
time: 1140 us; the launch traced here: 1120 us
  Pallas kernels  611 us (54%)
  starting transfers between devices  218 us (19%)
  waiting for transfers between devices  200 us (18%)
  local copies, waits for them, and re-layouts  76.6 us (7%)
  other arithmetic  14.9 us (1%)
    pallas_call x12, Pallas kernels, mlp_layer(): pl.pallas_call(mlp_kernel, grid_spec=pltpu.PrefetchScalarGridSpec(num_sca...  534 us
    ppermute x96, starting transfers between devices, send(): return lax.ppermute(x, axes, pairs)  212 us
    ppermute x96, waiting for transfers between devices, send(): return lax.ppermute(x, axes, pairs)  124 us
    pallas_call x12, Pallas kernels, update_group(): pl.pallas_call(update_kernel, grid_spec=pltpu.PrefetchScalarGridSpec(num_...  76.2 us
    ppermute x4, waiting for transfers between devices, device_step(): back[dt, dc] = lax.ppermute(cols[:, dc * part:(dc + 1) * part], axes, perm)  76.1 us
    dynamic_slice x1, local copies, waits for them, and re-layouts, device_step(): mine = lax.dynamic_slice_in_dim(runs, j, 1, axis=2).reshape(half, part)  27.3 us
  transfers between devices with their start and end apart: 101, of which 16 were waited for; matrix products, arithmetic and copies ran while one was open for 2% of the time, Pallas kernels for 50%

profile of v1, /device:TPU:0, one launch (start us, length us, event | category | flops | bytes accessed | tf_op | source)
XLA Modules:
  0.0 1124.9 jit_solution(13208978626331053474)
XLA Ops:
  0.7 9.2 reshape.156
  9.8 27.3 %dynamic-slice_reduce_fusion.3 = (bf16[480,8,128]{2,1,0:T(8,128)(2,1)S(1)}, bf16[480,8,128]{2,1,0:T(8,128)(2,1)S(1)}, bf16[480,8,128]{2,1,0:T(8,128)(2,1)S(1)}, bf16[480,8,128]{2,1,0:T(8,128)(2,1)S(1)}) fusion(bf16[480,8,4,128]{3,2,1,0:T(4,128)(2,1)} %reshape.156, s32[]{:T(128)S(6)} %select_n.97, s32[]{:T(128)S(6)} %select_n.99, s32[]{:T(128)S(6)} %select_n.98, ...), kind=kLoop, calls=%fused_computation.12 | loop fusion | bytes 7864336 | tf_op jit(solution)/shard_map/dynamic_slice | solution.py:198
  40.3 6.4 update.12
  46.6 6.3 update.13
  53.0 6.4 update.14
  59.4 6.6 collective-permute-start.10
  76.4 6.3 update.15
  82.7 34.2 %collective-permute-done.3 = bf16[480,1024]{1,0:T(8,128)(2,1)S(1)} collective-permute-done((bf16[480,1024]{1,0:T(8,128)(2,1)}, bf16[480,1024]{1,0:T(8,128)(2,1)S(1)}, u32[]{:S(2)}, u32[]{:S(2)}) %collective-permute-start.3) | collective-permute-done | bytes 983072 | tf_op jit(solution)/shard_map/ppermute | solution.py:177
  116.9 3.9 collective-permute-start.6
  120.8 16.0 %collective-permute-done.4 = bf16[480,1024]{1,0:T(8,128)(2,1)S(1)} collective-permute-done((bf16[480,1024]{1,0:T(8,128)(2,1)}, bf16[480,1024]{1,0:T(8,128)(2,1)S(1)}, u32[]{:S(2)}, u32[]{:S(2)}) %collective-permute-start.4) | collective-permute-done | bytes 983072 | tf_op jit(solution)/shard_map/ppermute | solution.py:177
  141.9 3.6 collective-permute-start.16
  147.2 6.3 update.16
  157.8 10.7 collective-permute-done.18
  177.7 6.3 update.17
  207.4 44.5 %shard_map.94.x_ref = bf16[2,2048,480]{2,1,0:T(8,128)(2,1)} custom-call(s32[8]{0:T(128)} %fusion.1.live_ref, bf16[2,2048,480]{2,1,0:T(8,128)(2,1)} %maximum_bitcast_fusion.x_ref, bf16[1,480,1280]{2,1,0:T(8,128)(2,1)} %get-tuple-element.114.refs_0_, bf16[1,480,1280]{2,1,0:T(8,128)(2,1)} %collective-permute-done.5.refs_1_, ...), custom_call_target="tpu_custom_call" | custom-call | flops 20132659200 | bytes 25165824 | tf_op jit(solution)/shard_map/pallas_call | solution.py:132
  262.8 6.4 update.18
  269.1 6.3 update.19
  275.5 5.7 collective-permute-done.34
  285.6 3.6 collective-permute-start.29
  294.7 44.5 %shard_map.95.x_ref = bf16[2,2048,480]{2,1,0:T(8,128)(2,1)} custom-call(s32[8]{0:T(128)} %fusion.1.live_ref, bf16[2,2048,480]{2,1,0:T(8,128)(2,1)} %shard_map.94.x_ref, bf16[1,480,1280]{2,1,0:T(8,128)(2,1)} %get-tuple-element.118.refs_0_, bf16[1,480,1280]{2,1,0:T(8,128)(2,1)} %collective-permute-done.12.refs_1_, bf16[1,480,1280]{2,1,0:T(8,128)(2,1)} %copy-done.32, ...), custom_call_target="tpu_custom_call" | custom-call | flops 20132659200 | bytes 25165824 | tf_op jit(solution)/shard_map/pallas_call | solution.py:132
  349.6 44.5 %shard_map.96.x_ref = bf16[2,2048,480]{2,1,0:T(8,128)(2,1)} custom-call(s32[8]{0:T(128)} %fusion.1.live_ref, bf16[2,2048,480]{2,1,0:T(8,128)(2,1)} %shard_map.95.x_ref, bf16[1,480,1280]{2,1,0:T(8,128)(2,1)} %get-tuple-element.122.refs_0_, bf16[1,480,1280]{2,1,0:T(8,128)(2,1)} %copy-done.38, bf16[1,480,1280]{2,1,0:T(8,128)(2,1)} %copy-done.24, ...), custom_call_target="tpu_custom_call" | custom-call | flops 20132659200 | bytes 25165824 | tf_op jit(solution)/shard_map/pallas_call | solution.py:132
  405.6 6.3 update.20
  414.3 10.2 collective-permute-done.50
  426.5 4.4 collective-permute-start.58
  434.8 44.5 %shard_map.97.x_ref = bf16[2,2048,480]{2,1,0:T(8,128)(2,1)} custom-call(s32[8]{0:T(128)} %fusion.1.live_ref, bf16[2,2048,480]{2,1,0:T(8,128)(2,1)} %shard_map.96.x_ref, bf16[1,480,1280]{2,1,0:T(8,128)(2,1)} %get-tuple-element.126.refs_0_, bf16[1,480,1280]{2,1,0:T(8,128)(2,1)} %collective-permute-done.28.refs_1_, ...), custom_call_target="tpu_custom_call" | custom-call | flops 20132659200 | bytes 25165824 | tf_op jit(solution)/shard_map/pallas_call | solution.py:132
  491.3 6.4 update.21
  497.7 6.4 update.22
  504.1 5.5 collective-permute-done.53.refs_2_
  522.9 44.5 %shard_map.98.x_ref = bf16[2,2048,480]{2,1,0:T(8,128)(2,1)} custom-call(s32[8]{0:T(128)} %fusion.1.live_ref, bf16[2,2048,480]{2,1,0:T(8,128)(2,1)} %shard_map.97.x_ref, bf16[1,480,1280]{2,1,0:T(8,128)(2,1)} %get-tuple-element.132.refs_0_, bf16[1,480,1280]{2,1,0:T(8,128)(2,1)} %copy-done.31, bf16[1,480,1280]{2,1,0:T(8,128)(2,1)} %collective-permute-done.37.refs_2_, ...), custom_call_target="tpu_custom_call" | custom-call | flops 20132659200 | bytes 25165824 | tf_op jit(solution)/shard_map/pallas_call | solution.py:132
  577.4 44.6 %shard_map.99.x_ref = bf16[2,2048,480]{2,1,0:T(8,128)(2,1)} custom-call(s32[8]{0:T(128)} %fusion.1.live_ref, bf16[2,2048,480]{2,1,0:T(8,128)(2,1)} %shard_map.98.x_ref, bf16[1,480,1280]{2,1,0:T(8,128)(2,1)} %get-tuple-element.138.refs_0_, bf16[1,480,1280]{2,1,0:T(8,128)(2,1)} %copy-done.39, bf16[1,480,1280]{2,1,0:T(8,128)(2,1)} %collective-permute-done.45.refs_2_, ...), custom_call_target="tpu_custom_call" | custom-call | flops 20132659200 | bytes 25165824 | tf_op jit(solution)/shard_map/pallas_call | solution.py:132
  632.6 6.4 update.23
  641.2 11.6 %collective-permute-done.74 = bf16[1,480,1280]{2,1,0:T(8,128)(2,1)} collective-permute-done((bf16[1,480,1280]{2,1,0:T(8,128)(2,1)}, bf16[1,480,1280]{2,1,0:T(8,128)(2,1)}, u32[]{:S(2)}, u32[]{:S(2)}) %collective-permute-start.74) | collective-permute-done | bytes 1228832 | tf_op jit(solution)/shard_map/ppermute | solution.py:177
  652.8 4.6 collective-permute-start.82
  663.5 44.5 %shard_map.100.x_ref = bf16[2,2048,480]{2,1,0:T(8,128)(2,1)} custom-call(s32[8]{0:T(128)} %fusion.1.live_ref, bf16[2,2048,480]{2,1,0:T(8,128)(2,1)} %shard_map.99.x_ref, bf16[1,480,1280]{2,1,0:T(8,128)(2,1)} %get-tuple-element.144.refs_0_, bf16[1,480,1280]{2,1,0:T(8,128)(2,1)} %collective-permute-done.52.refs_1_, ...), custom_call_target="tpu_custom_call" | custom-call | flops 20132659200 | bytes 25165824 | tf_op jit(solution)/shard_map/pallas_call | solution.py:132
  719.1 44.7 %shard_map.101.x_ref = bf16[2,2048,480]{2,1,0:T(8,128)(2,1)} custom-call(s32[8]{0:T(128)} %fusion.1.live_ref, bf16[2,2048,480]{2,1,0:T(8,128)(2,1)} %shard_map.100.x_ref, bf16[1,480,1280]{2,1,0:T(8,128)(2,1)} %get-tuple-element.150.refs_0_, bf16[1,480,1280]{2,1,0:T(8,128)(2,1)} %collective-permute-done.60.refs_1_, bf16[1,480,1280]{2,1,0:T(8,128)(2,1)} %copy-done.23, ...), custom_call_target="tpu_custom_call" | custom-call | flops 20132659200 | bytes 25165824 | tf_op jit(solution)/shard_map/pallas_call | solution.py:132
  766.0 3.5 collective-permute-start.85
  776.5 20.7 %collective-permute-done.85.refs_2_ = bf16[1,480,1280]{2,1,0:T(8,128)(2,1)S(1)} collective-permute-done((bf16[1,480,1280]{2,1,0:T(8,128)(2,1)S(1)}, bf16[1,480,1280]{2,1,0:T(8,128)(2,1)S(1)}, u32[]{:S(2)}, u32[]{:S(2)}) %collective-permute-start.85) | collective-permute-done | bytes 1228832 | tf_op jit(solution)/shard_map/ppermute | solution.py:177
  806.9 44.5 %shard_map.102.x_ref = bf16[2,2048,480]{2,1,0:T(8,128)(2,1)} custom-call(s32[8]{0:T(128)} %fusion.1.live_ref, bf16[2,2048,480]{2,1,0:T(8,128)(2,1)} %shard_map.101.x_ref, bf16[1,480,1280]{2,1,0:T(8,128)(2,1)} %get-tuple-element.156.refs_0_, bf16[1,480,1280]{2,1,0:T(8,128)(2,1)} %collective-permute-done.68.refs_1_, ...), custom_call_target="tpu_custom_call" | custom-call | flops 20132659200 | bytes 25165824 | tf_op jit(solution)/shard_map/pallas_call | solution.py:132
  855.9 3.5 collective-permute-start.92
  863.9 44.5 %shard_map.103.x_ref = bf16[2,2048,480]{2,1,0:T(8,128)(2,1)} custom-call(s32[8]{0:T(128)} %fusion.1.live_ref, bf16[2,2048,480]{2,1,0:T(8,128)(2,1)} %shard_map.102.x_ref, bf16[1,480,1280]{2,1,0:T(8,128)(2,1)} %get-tuple-element.162.refs_0_, bf16[1,480,1280]{2,1,0:T(8,128)(2,1)} %collective-permute-done.76.refs_1_, bf16[1,480,1280]{2,1,0:T(8,128)(2,1)} %copy-done.25, ...), custom_call_target="tpu_custom_call" | custom-call | flops 20132659200 | bytes 25165824 | tf_op jit(solution)/shard_map/pallas_call | solution.py:132
  914.1 44.5 %shard_map.104.x_ref = bf16[2,2048,480]{2,1,0:T(8,128)(2,1)} custom-call(s32[8]{0:T(128)} %fusion.1.live_ref, bf16[2,2048,480]{2,1,0:T(8,128)(2,1)} %shard_map.103.x_ref, bf16[1,480,1280]{2,1,0:T(8,128)(2,1)} %get-tuple-element.168.refs_0_, bf16[1,480,1280]{2,1,0:T(8,128)(2,1)} %collective-permute-done.84.refs_1_, bf16[1,480,1280]{2,1,0:T(8,128)(2,1)} %copy-done.27, ...), custom_call_target="tpu_custom_call" | custom-call | flops 20132659200 | bytes 25165824 | tf_op jit(solution)/shard_map/pallas_call | solution.py:132
  965.7 44.5 %shard_map.105 = bf16[2,2048,480]{2,1,0:T(8,128)(2,1)} custom-call(s32[8]{0:T(128)} %fusion.1.live_ref, bf16[2,2048,480]{2,1,0:T(8,128)(2,1)} %shard_map.104.x_ref, bf16[1,480,1280]{2,1,0:T(8,128)(2,1)} %get-tuple-element.173.refs_0_, bf16[1,480,1280]{2,1,0:T(8,128)(2,1)} %copy-done.41, bf16[1,480,1280]{2,1,0:T(8,128)(2,1)} %copy-done.36, ...), custom_call_target="tpu_custom_call" | custom-call | flops 20132659200 | bytes 25165824 | tf_op jit(solution)/shard_map/pallas_call | solution.py:132
  1026.8 13.2 %collective-permute-done.100 = bf16[480,1024]{1,0:T(8,128)(2,1)} collective-permute-done((bf16[480,1024]{1,0:T(8,128)(2,1)}, bf16[480,1024]{1,0:T(8,128)(2,1)}, u32[]{:S(2)}, u32[]{:S(2)}) %collective-permute-start.100) | collective-permute-done | bytes 983072 | tf_op jit(solution)/shard_map/ppermute | solution.py:265
  1040.0 41.8 %collective-permute-done.97 = bf16[480,1024]{1,0:T(8,128)(2,1)S(1)} collective-permute-done((bf16[480,1024]{1,0:T(8,128)(2,1)}, bf16[480,1024]{1,0:T(8,128)(2,1)S(1)}, u32[]{:S(2)}, u32[]{:S(2)}) %collective-permute-start.97) | collective-permute-done | bytes 983072 | tf_op jit(solution)/shard_map/ppermute | solution.py:265
  1081.8 21.0 %collective-permute-done.98 = bf16[480,1024]{1,0:T(8,128)(2,1)S(1)} collective-permute-done((bf16[480,1024]{1,0:T(8,128)(2,1)}, bf16[480,1024]{1,0:T(8,128)(2,1)S(1)}, u32[]{:S(2)}, u32[]{:S(2)}) %collective-permute-start.98) | collective-permute-done | bytes 983072 | tf_op jit(solution)/shard_map/ppermute | solution.py:265
  1106.0 7.0 copy.49
  1112.9 7.4 reshape.161
  1120.3 4.3 select_bitcast_fusion
  (299 shorter events, 230.8 us)
Async XLA Ops:
  59.4 82.5 %collective-permute-start.10 = (bf16[1,480,1280]{2,1,0:T(8,128)(2,1)}, bf16[1,480,1280]{2,1,0:T(8,128)(2,1)}, u32[]{:S(2)}, u32[]{:S(2)}) collective-permute-start(bf16[1,480,1280]{2,1,0:T(8,128)(2,1)} %get-tuple-element.116.refs_4_), channel_id=1, source_target_pairs={{0,4},{1,5},{2,6},{3,7}} | collective-permute-start | bytes 3686408 | tf_op jit(solution)/shard_map/ppermute | solution.py:177
  66.0 79.6 %collective-permute-start.9 = (bf16[1,480,1280]{2,1,0:T(8,128)(2,1)}, bf16[1,480,1280]{2,1,0:T(8,128)(2,1)}, u32[]{:S(2)}, u32[]{:S(2)}) collective-permute-start(bf16[1,480,1280]{2,1,0:T(8,128)(2,1)} %get-tuple-element.115.refs_4_), channel_id=1, source_target_pairs={{0,2},{1,3},{2,0},{3,1}} | collective-permute-start | bytes 3686408 | tf_op jit(solution)/shard_map/ppermute | solution.py:177
  73.3 63.5 %collective-permute-start.4 = (bf16[480,1024]{1,0:T(8,128)(2,1)}, bf16[480,1024]{1,0:T(8,128)(2,1)S(1)}, u32[]{:S(2)}, u32[]{:S(2)}) collective-permute-start(bf16[480,1024]{1,0:T(8,128)(2,1)} %bitcast.57), channel_id=1, source_target_pairs={{4,1},{5,0},{6,3},{7,2}} | collective-permute-start | bytes 2949128 | tf_op jit(solution)/shard_map/ppermute | solution.py:177
  74.6 64.9 %collective-permute-start.1 = (bf16[480,1024]{1,0:T(8,128)(2,1)}, bf16[480,1024]{1,0:T(8,128)(2,1)S(1)}, u32[]{:S(2)}, u32[]{:S(2)}) collective-permute-start(bf16[480,1024]{1,0:T(8,128)(2,1)} %bitcast.60), channel_id=1, source_target_pairs={{4,2},{5,3},{6,0},{7,1}} | collective-permute-start | bytes 2949128 | tf_op jit(solution)/shard_map/ppermute | solution.py:177
  195.8 56.1 %collective-permute-start.13 = (bf16[1,480,1280]{2,1,0:T(8,128)(2,1)S(1)}, bf16[1,480,1280]{2,1,0:T(8,128)(2,1)S(1)}, u32[]{:S(2)}, u32[]{:S(2)}) collective-permute-start(bf16[1,480,1280]{2,1,0:T(8,128)(2,1)S(1)} %copy-done.17), channel_id=1, source_target_pairs={{0,2},{1,3},{2,0},{3,1}} | collective-permute-start | bytes 3686408 | tf_op jit(solution)/shard_map/ppermute | solution.py:177
  199.2 55.1 %collective-permute-start.12 = (bf16[1,480,1280]{2,1,0:T(8,128)(2,1)S(1)}, bf16[1,480,1280]{2,1,0:T(8,128)(2,1)}, u32[]{:S(2)}, u32[]{:S(2)}) collective-permute-start(bf16[1,480,1280]{2,1,0:T(8,128)(2,1)S(1)} %copy-done.17), channel_id=1, source_target_pairs={{0,1},{1,0},{2,3},{3,2}} | collective-permute-start | bytes 3686408 | tf_op jit(solution)/shard_map/ppermute | solution.py:177
  201.4 54.9 %collective-permute-start.15 = (bf16[1,480,1280]{2,1,0:T(8,128)(2,1)S(1)}, bf16[1,480,1280]{2,1,0:T(8,128)(2,1)}, u32[]{:S(2)}, u32[]{:S(2)}) collective-permute-start(bf16[1,480,1280]{2,1,0:T(8,128)(2,1)S(1)} %copy-done.18), channel_id=1, source_target_pairs={{0,1},{1,0},{2,3},{3,2}} | collective-permute-start | bytes 3686408 | tf_op jit(solution)/shard_map/ppermute | solution.py:177
  203.6 55.1 %collective-permute-start.21 = (bf16[1,480,1280]{2,1,0:T(8,128)(2,1)S(1)}, bf16[1,480,1280]{2,1,0:T(8,128)(2,1)S(1)}, u32[]{:S(2)}, u32[]{:S(2)}) collective-permute-start(bf16[1,480,1280]{2,1,0:T(8,128)(2,1)S(1)} %copy-done.16), channel_id=1, source_target_pairs={{0,2},{1,3},{2,0},{3,1}} | collective-permute-start | bytes 3686408 | tf_op jit(solution)/shard_map/ppermute | solution.py:177
  206.1 55.4 %collective-permute-start.24 = (bf16[1,480,1280]{2,1,0:T(8,128)(2,1)}, bf16[1,480,1280]{2,1,0:T(8,128)(2,1)}, u32[]{:S(2)}, u32[]{:S(2)}) collective-permute-start(bf16[1,480,1280]{2,1,0:T(8,128)(2,1)} %collective-permute-done.17), channel_id=1, source_target_pairs={{4,0},{5,1},{6,2},{7,3}} | collective-permute-start | bytes 3686408 | tf_op jit(solution)/shard_map/ppermute | solution.py:177
  281.2 60.5 %collective-permute-start.20 = (bf16[1,480,1280]{2,1,0:T(8,128)(2,1)S(1)}, bf16[1,480,1280]{2,1,0:T(8,128)(2,1)S(1)}, u32[]{:S(2)}, u32[]{:S(2)}) collective-permute-start(bf16[1,480,1280]{2,1,0:T(8,128)(2,1)S(1)} %copy-done.16), channel_id=1, source_target_pairs={{0,1},{1,0},{2,3},{3,2}} | collective-permute-start | bytes 3686408 | tf_op jit(solution)/shard_map/ppermute | solution.py:177
  283.1 60.9 %collective-permute-start.23 = (bf16[1,480,1280]{2,1,0:T(8,128)(2,1)}, bf16[1,480,1280]{2,1,0:T(8,128)(2,1)}, u32[]{:S(2)}, u32[]{:S(2)}) collective-permute-start(bf16[1,480,1280]{2,1,0:T(8,128)(2,1)} %get-tuple-element.116.refs_4_), channel_id=1, source_target_pairs={{0,1},{1,0},{2,3},{3,2}} | collective-permute-start | bytes 3686408 | tf_op jit(solution)/shard_map/ppermute | solution.py:177
  289.2 58.3 %collective-permute-start.22 = (bf16[1,480,1280]{2,1,0:T(8,128)(2,1)}, bf16[1,480,1280]{2,1,0:T(8,128)(2,1)}, u32[]{:S(2)}, u32[]{:S(2)}) collective-permute-start(bf16[1,480,1280]{2,1,0:T(8,128)(2,1)} %copy-done.24), channel_id=1, source_target_pairs={{0,1},{1,0},{2,3},{3,2}} | collective-permute-start | bytes 3686408 | tf_op jit(solution)/shard_map/ppermute | solution.py:177
  292.6 55.6 %collective-permute-start.27 = (bf16[1,480,1280]{2,1,0:T(8,128)(2,1)}, bf16[1,480,1280]{2,1,0:T(8,128)(2,1)}, u32[]{:S(2)}, u32[]{:S(2)}) collective-permute-start(bf16[1,480,1280]{2,1,0:T(8,128)(2,1)} %collective-permute-done.24.refs_6_), channel_id=1, source_target_pairs={{0,1},{1,0},{2,3},{3,2}} | collective-permute-start | bytes 3686408 | tf_op jit(solution)/shard_map/ppermute | solution.py:177
  339.2 59.2 %collective-permute-start.28 = (bf16[1,480,1280]{2,1,0:T(8,128)(2,1)}, bf16[1,480,1280]{2,1,0:T(8,128)(2,1)}, u32[]{:S(2)}, u32[]{:S(2)}) collective-permute-start(bf16[1,480,1280]{2,1,0:T(8,128)(2,1)} %get-tuple-element.126.refs_0_), channel_id=1, source_target_pairs={{0,1},{1,0},{2,3},{3,2}} | collective-permute-start | bytes 3686408 | tf_op jit(solution)/shard_map/ppermute | solution.py:177
  348.3 55.6 %collective-permute-start.40 = (bf16[1,480,1280]{2,1,0:T(8,128)(2,1)}, bf16[1,480,1280]{2,1,0:T(8,128)(2,1)}, u32[]{:S(2)}, u32[]{:S(2)}) collective-permute-start(bf16[1,480,1280]{2,1,0:T(8,128)(2,1)} %collective-permute-done.33), channel_id=1, source_target_pairs={{4,0},{5,1},{6,2},{7,3}} | collective-permute-start | bytes 3686408 | tf_op jit(solution)/shard_map/ppermute | solution.py:177
  411.9 67.4 %collective-permute-start.36 = (bf16[1,480,1280]{2,1,0:T(8,128)(2,1)S(1)}, bf16[1,480,1280]{2,1,0:T(8,128)(2,1)S(1)}, u32[]{:S(2)}, u32[]{:S(2)}) collective-permute-start(bf16[1,480,1280]{2,1,0:T(8,128)(2,1)S(1)} %copy-done.5), channel_id=1, source_target_pairs={{0,1},{1,0},{2,3},{3,2}} | collective-permute-start | bytes 3686408 | tf_op jit(solution)/shard_map/ppermute | solution.py:177
  424.6 58.1 %collective-permute-start.39 = (bf16[1,480,1280]{2,1,0:T(8,128)(2,1)}, bf16[1,480,1280]{2,1,0:T(8,128)(2,1)S(1)}, u32[]{:S(2)}, u32[]{:S(2)}) collective-permute-start(bf16[1,480,1280]{2,1,0:T(8,128)(2,1)} %get-tuple-element.124.refs_4_), channel_id=1, source_target_pairs={{0,1},{1,0},{2,3},{3,2}} | collective-permute-start | bytes 3686408 | tf_op jit(solution)/shard_map/ppermute | solution.py:177
  426.5 59.2 %collective-permute-start.58 = (bf16[1,480,1280]{2,1,0:T(8,128)(2,1)}, bf16[1,480,1280]{2,1,0:T(8,128)(2,1)}, u32[]{:S(2)}, u32[]{:S(2)}) collective-permute-start(bf16[1,480,1280]{2,1,0:T(8,128)(2,1)} %get-tuple-element.148.refs_4_), channel_id=1, source_target_pairs={{0,4},{1,5},{2,6},{3,7}} | collective-permute-start | bytes 3686408 | tf_op jit(solution)/shard_map/ppermute | solution.py:177
  430.9 57.2 %collective-permute-start.45 = (bf16[1,480,1280]{2,1,0:T(8,128)(2,1)}, bf16[1,480,1280]{2,1,0:T(8,128)(2,1)}, u32[]{:S(2)}, u32[]{:S(2)}) collective-permute-start(bf16[1,480,1280]{2,1,0:T(8,128)(2,1)} %get-tuple-element.138.refs_0_), channel_id=1, source_target_pairs={{0,2},{1,3},{2,0},{3,1}} | collective-permute-start | bytes 3686408 | tf_op jit(solution)/shard_map/ppermute | solution.py:177
  433.5 56.3 %collective-permute-start.48 = (bf16[1,480,1280]{2,1,0:T(8,128)(2,1)}, bf16[1,480,1280]{2,1,0:T(8,128)(2,1)}, u32[]{:S(2)}, u32[]{:S(2)}) collective-permute-start(bf16[1,480,1280]{2,1,0:T(8,128)(2,1)} %copy-done.30), channel_id=1, source_target_pairs={{4,0},{5,1},{6,2},{7,3}} | collective-permute-start | bytes 3686408 | tf_op jit(solution)/shard_map/ppermute | solution.py:177
  509.6 57.8 %collective-permute-start.44 = (bf16[1,480,1280]{2,1,0:T(8,128)(2,1)S(1)}, bf16[1,480,1280]{2,1,0:T(8,128)(2,1)S(1)}, u32[]{:S(2)}, u32[]{:S(2)}) collective-permute-start(bf16[1,480,1280]{2,1,0:T(8,128)(2,1)S(1)} %copy-done.6), channel_id=1, source_target_pairs={{0,1},{1,0},{2,3},{3,2}} | collective-permute-start | bytes 3686408 | tf_op jit(solution)/shard_map/ppermute | solution.py:177
  511.5 58.3 %collective-permute-start.47 = (bf16[1,480,1280]{2,1,0:T(8,128)(2,1)}, bf16[1,480,1280]{2,1,0:T(8,128)(2,1)}, u32[]{:S(2)}, u32[]{:S(2)}) collective-permute-start(bf16[1,480,1280]{2,1,0:T(8,128)(2,1)} %get-tuple-element.130.refs_4_), channel_id=1, source_target_pairs={{0,1},{1,0},{2,3},{3,2}} | collective-permute-start | bytes 3686408 | tf_op jit(solution)/shard_map/ppermute | solution.py:177
  514.0 57.8 %collective-permute-start.66 = (bf16[1,480,1280]{2,1,0:T(8,128)(2,1)}, bf16[1,480,1280]{2,1,0:T(8,128)(2,1)}, u32[]{:S(2)}, u32[]{:S(2)}) collective-permute-start(bf16[1,480,1280]{2,1,0:T(8,128)(2,1)} %get-tuple-element.154.refs_4_), channel_id=1, source_target_pairs={{0,4},{1,5},{2,6},{3,7}} | collective-permute-start | bytes 3686408 | tf_op jit(solution)/shard_map/ppermute | solution.py:177
  516.7 57.7 %collective-permute-start.46 = (bf16[1,480,1280]{2,1,0:T(8,128)(2,1)}, bf16[1,480,1280]{2,1,0:T(8,128)(2,1)}, u32[]{:S(2)}, u32[]{:S(2)}) collective-permute-start(bf16[1,480,1280]{2,1,0:T(8,128)(2,1)} %collective-permute-done.45.refs_2_), channel_id=1, source_target_pairs={{0,1},{1,0},{2,3},{3,2}} | collective-permute-start | bytes 3686408 | tf_op jit(solution)/shard_map/ppermute | solution.py:177
  521.0 55.2 %collective-permute-start.51 = (bf16[1,480,1280]{2,1,0:T(8,128)(2,1)}, bf16[1,480,1280]{2,1,0:T(8,128)(2,1)}, u32[]{:S(2)}, u32[]{:S(2)}) collective-permute-start(bf16[1,480,1280]{2,1,0:T(8,128)(2,1)} %collective-permute-done.48.refs_6_), channel_id=1, source_target_pairs={{0,1},{1,0},{2,3},{3,2}} | collective-permute-start | bytes 3686408 | tf_op jit(solution)/shard_map/ppermute | solution.py:177
  567.4 56.8 %collective-permute-start.52 = (bf16[1,480,1280]{2,1,0:T(8,128)(2,1)S(1)}, bf16[1,480,1280]{2,1,0:T(8,128)(2,1)}, u32[]{:S(2)}, u32[]{:S(2)}) collective-permute-start(bf16[1,480,1280]{2,1,0:T(8,128)(2,1)S(1)} %copy-done.8), channel_id=1, source_target_pairs={{0,1},{1,0},{2,3},{3,2}} | collective-permute-start | bytes 3686408 | tf_op jit(solution)/shard_map/ppermute | solution.py:177
  569.9 56.6 %collective-permute-start.55 = (bf16[1,480,1280]{2,1,0:T(8,128)(2,1)S(1)}, bf16[1,480,1280]{2,1,0:T(8,128)(2,1)}, u32[]{:S(2)}, u32[]{:S(2)}) collective-permute-start(bf16[1,480,1280]{2,1,0:T(8,128)(2,1)S(1)} %copy-done.10), channel_id=1, source_target_pairs={{0,1},{1,0},{2,3},{3,2}} | collective-permute-start | bytes 3686408 | tf_op jit(solution)/shard_map/ppermute | solution.py:177
  574.3 54.4 %collective-permute-start.65 = (bf16[1,480,1280]{2,1,0:T(8,128)(2,1)}, bf16[1,480,1280]{2,1,0:T(8,128)(2,1)}, u32[]{:S(2)}, u32[]{:S(2)}) collective-permute-start(bf16[1,480,1280]{2,1,0:T(8,128)(2,1)} %collective-permute-done.58), channel_id=1, source_target_pairs={{4,6},{5,7},{6,4},{7,5}} | collective-permute-start | bytes 3686408 | tf_op jit(solution)/shard_map/ppermute | solution.py:177
  576.1 54.7 %collective-permute-start.64 = (bf16[1,480,1280]{2,1,0:T(8,128)(2,1)}, bf16[1,480,1280]{2,1,0:T(8,128)(2,1)S(1)}, u32[]{:S(2)}, u32[]{:S(2)}) collective-permute-start(bf16[1,480,1280]{2,1,0:T(8,128)(2,1)} %collective-permute-done.57), channel_id=1, source_target_pairs={{4,0},{5,1},{6,2},{7,3}} | collective-permute-start | bytes 3686408 | tf_op jit(solution)/shard_map/ppermute | solution.py:177
  639.0 69.0 %collective-permute-start.63 = (bf16[1,480,1280]{2,1,0:T(8,128)(2,1)S(1)}, bf16[1,480,1280]{2,1,0:T(8,128)(2,1)S(1)}, u32[]{:S(2)}, u32[]{:S(2)}) collective-permute-start(bf16[1,480,1280]{2,1,0:T(8,128)(2,1)S(1)} %copy-done.4), channel_id=1, source_target_pairs={{0,1},{1,0},{2,3},{3,2}} | collective-permute-start | bytes 3686408 | tf_op jit(solution)/shard_map/ppermute | solution.py:177
  652.8 58.5 %collective-permute-start.82 = (bf16[1,480,1280]{2,1,0:T(8,128)(2,1)}, bf16[1,480,1280]{2,1,0:T(8,128)(2,1)S(1)}, u32[]{:S(2)}, u32[]{:S(2)}) collective-permute-start(bf16[1,480,1280]{2,1,0:T(8,128)(2,1)} %get-tuple-element.166.refs_4_), channel_id=1, source_target_pairs={{0,4},{1,5},{2,6},{3,7}} | collective-permute-start | bytes 3686408 | tf_op jit(solution)/shard_map/ppermute | solution.py:177
  657.4 55.8 %collective-permute-start.67 = (bf16[1,480,1280]{2,1,0:T(8,128)(2,1)}, bf16[1,480,1280]{2,1,0:T(8,128)(2,1)}, u32[]{:S(2)}, u32[]{:S(2)}) collective-permute-start(bf16[1,480,1280]{2,1,0:T(8,128)(2,1)} %copy-done.26), channel_id=1, source_target_pairs={{0,1},{1,0},{2,3},{3,2}} | collective-permute-start | bytes 3686408 | tf_op jit(solution)/shard_map/ppermute | solution.py:177
  659.3 56.8 %collective-permute-start.62 = (bf16[1,480,1280]{2,1,0:T(8,128)(2,1)}, bf16[1,480,1280]{2,1,0:T(8,128)(2,1)}, u32[]{:S(2)}, u32[]{:S(2)}) collective-permute-start(bf16[1,480,1280]{2,1,0:T(8,128)(2,1)} %copy-done.23), channel_id=1, source_target_pairs={{0,1},{1,0},{2,3},{3,2}} | collective-permute-start | bytes 3686408 | tf_op jit(solution)/shard_map/ppermute | solution.py:177
  661.8 56.0 %collective-permute-start.72 = (bf16[1,480,1280]{2,1,0:T(8,128)(2,1)}, bf16[1,480,1280]{2,1,0:T(8,128)(2,1)}, u32[]{:S(2)}, u32[]{:S(2)}) collective-permute-start(bf16[1,480,1280]{2,1,0:T(8,128)(2,1)} %collective-permute-done.65), channel_id=1, source_target_pairs={{4,0},{5,1},{6,2},{7,3}} | collective-permute-start | bytes 3686408 | tf_op jit(solution)/shard_map/ppermute | solution.py:177
  708.0 55.8 %collective-permute-start.69 = (bf16[1,480,1280]{2,1,0:T(8,128)(2,1)S(1)}, bf16[1,480,1280]{2,1,0:T(8,128)(2,1)}, u32[]{:S(2)}, u32[]{:S(2)}) collective-permute-start(bf16[1,480,1280]{2,1,0:T(8,128)(2,1)S(1)} %copy-done.11), channel_id=1, source_target_pairs={{0,2},{1,3},{2,0},{3,1}} | collective-permute-start | bytes 3686408 | tf_op jit(solution)/shard_map/ppermute | solution.py:177
  711.3 54.6 %collective-permute-start.68 = (bf16[1,480,1280]{2,1,0:T(8,128)(2,1)S(1)}, bf16[1,480,1280]{2,1,0:T(8,128)(2,1)}, u32[]{:S(2)}, u32[]{:S(2)}) collective-permute-start(bf16[1,480,1280]{2,1,0:T(8,128)(2,1)S(1)} %copy-done.11), channel_id=1, source_target_pairs={{0,1},{1,0},{2,3},{3,2}} | collective-permute-start | bytes 3686408 | tf_op jit(solution)/shard_map/ppermute | solution.py:177
  713.3 56.1 %collective-permute-start.77 = (bf16[1,480,1280]{2,1,0:T(8,128)(2,1)S(1)}, bf16[1,480,1280]{2,1,0:T(8,128)(2,1)S(1)}, u32[]{:S(2)}, u32[]{:S(2)}) collective-permute-start(bf16[1,480,1280]{2,1,0:T(8,128)(2,1)S(1)} %copy-done.14), channel_id=1, source_target_pairs={{0,2},{1,3},{2,0},{3,1}} | collective-permute-start | bytes 3686408 | tf_op jit(solution)/shard_map/ppermute | solution.py:177
  774.6 79.3 %collective-permute-start.76 = (bf16[1,480,1280]{2,1,0:T(8,128)(2,1)S(1)}, bf16[1,480,1280]{2,1,0:T(8,128)(2,1)}, u32[]{:S(2)}, u32[]{:S(2)}) collective-permute-start(bf16[1,480,1280]{2,1,0:T(8,128)(2,1)S(1)} %copy-done.14), channel_id=1, source_target_pairs={{0,1},{1,0},{2,3},{3,2}} | collective-permute-start | bytes 3686408 | tf_op jit(solution)/shard_map/ppermute | solution.py:177
  797.2 58.7 %collective-permute-start.79 = (bf16[1,480,1280]{2,1,0:T(8,128)(2,1)S(1)}, bf16[1,480,1280]{2,1,0:T(8,128)(2,1)}, u32[]{:S(2)}, u32[]{:S(2)}) collective-permute-start(bf16[1,480,1280]{2,1,0:T(8,128)(2,1)S(1)} %copy-done.15), channel_id=1, source_target_pairs={{0,1},{1,0},{2,3},{3,2}} | collective-permute-start | bytes 3686408 | tf_op jit(solution)/shard_map/ppermute | solution.py:177
  800.2 59.2 %collective-permute-start.78 = (bf16[1,480,1280]{2,1,0:T(8,128)(2,1)S(1)}, bf16[1,480,1280]{2,1,0:T(8,128)(2,1)}, u32[]{:S(2)}, u32[]{:S(2)}) collective-permute-start(bf16[1,480,1280]{2,1,0:T(8,128)(2,1)S(1)} %collective-permute-done.77.refs_2_), channel_id=1, source_target_pairs={{0,1},{1,0},{2,3},{3,2}} | collective-permute-start | bytes 3686408 | tf_op jit(solution)/shard_map/ppermute | solution.py:177
  805.0 56.5 %collective-permute-start.83 = (bf16[1,480,1280]{2,1,0:T(8,128)(2,1)}, bf16[1,480,1280]{2,1,0:T(8,128)(2,1)}, u32[]{:S(2)}, u32[]{:S(2)}) collective-permute-start(bf16[1,480,1280]{2,1,0:T(8,128)(2,1)} %collective-permute-done.80.refs_6_), channel_id=1, source_target_pairs={{0,1},{1,0},{2,3},{3,2}} | collective-permute-start | bytes 3686408 | tf_op jit(solution)/shard_map/ppermute | solution.py:177
  851.5 56.9 %collective-permute-start.84 = (bf16[1,480,1280]{2,1,0:T(8,128)(2,1)S(1)}, bf16[1,480,1280]{2,1,0:T(8,128)(2,1)}, u32[]{:S(2)}, u32[]{:S(2)}) collective-permute-start(bf16[1,480,1280]{2,1,0:T(8,128)(2,1)S(1)} %copy-done.13), channel_id=1, source_target_pairs={{0,1},{1,0},{2,3},{3,2}} | collective-permute-start | bytes 3686408 | tf_op jit(solution)/shard_map/ppermute | solution.py:177
  853.9 56.6 %collective-permute-start.87 = (bf16[1,480,1280]{2,1,0:T(8,128)(2,1)}, bf16[1,480,1280]{2,1,0:T(8,128)(2,1)}, u32[]{:S(2)}, u32[]{:S(2)}) collective-permute-start(bf16[1,480,1280]{2,1,0:T(8,128)(2,1)} %get-tuple-element.160.refs_4_), channel_id=1, source_target_pairs={{0,1},{1,0},{2,3},{3,2}} | collective-permute-start | bytes 3686408 | tf_op jit(solution)/shard_map/ppermute | solution.py:177
  855.9 104.8 %collective-permute-start.92 = (bf16[1,480,1280]{2,1,0:T(8,128)(2,1)S(1)}, bf16[1,480,1280]{2,1,0:T(8,128)(2,1)S(1)}, u32[]{:S(2)}, u32[]{:S(2)}) collective-permute-start(bf16[1,480,1280]{2,1,0:T(8,128)(2,1)S(1)} %copy-done.19), channel_id=1, source_target_pairs={{0,2},{1,3},{2,0},{3,1}} | collective-permute-start | bytes 3686408 | tf_op jit(solution)/shard_map/ppermute | solution.py:177
  908.4 54.6 %collective-permute-start.91 = (bf16[1,480,1280]{2,1,0:T(8,128)(2,1)S(1)}, bf16[1,480,1280]{2,1,0:T(8,128)(2,1)S(1)}, u32[]{:S(2)}, u32[]{:S(2)}) collective-permute-start(bf16[1,480,1280]{2,1,0:T(8,128)(2,1)S(1)} %copy-done.19), channel_id=1, source_target_pairs={{0,1},{1,0},{2,3},{3,2}} | collective-permute-start | bytes 3686408 | tf_op jit(solution)/shard_map/ppermute | solution.py:177
  1019.8 62.1 %collective-permute-start.97 = (bf16[480,1024]{1,0:T(8,128)(2,1)}, bf16[480,1024]{1,0:T(8,128)(2,1)S(1)}, u32[]{:S(2)}, u32[]{:S(2)}) collective-permute-start(bf16[480,1024]{1,0:T(8,128)(2,1)} %copy.45), channel_id=1, source_target_pairs={{0,4},{1,5},{2,6},{3,7}} | collective-permute-start | bytes 2949128 | tf_op jit(solution)/shard_map/ppermute | solution.py:265
  1022.5 80.4 %collective-permute-start.98 = (bf16[480,1024]{1,0:T(8,128)(2,1)}, bf16[480,1024]{1,0:T(8,128)(2,1)S(1)}, u32[]{:S(2)}, u32[]{:S(2)}) collective-permute-start(bf16[480,1024]{1,0:T(8,128)(2,1)} %copy.46), channel_id=1, source_target_pairs={{0,5},{1,4},{2,7},{3,6}} | collective-permute-start | bytes 2949128 | tf_op jit(solution)/shard_map/ppermute | solution.py:265
  1025.2 77.7 %collective-permute-start.99 = (bf16[480,1024]{1,0:T(8,128)(2,1)}, bf16[480,1024]{1,0:T(8,128)(2,1)S(1)}, u32[]{:S(2)}, u32[]{:S(2)}) collective-permute-start(bf16[480,1024]{1,0:T(8,128)(2,1)} %copy.47), channel_id=1, source_target_pairs={{0,6},{1,7},{2,4},{3,5}} | collective-permute-start | bytes 2949128 | tf_op jit(solution)/shard_map/ppermute | solution.py:265
  (98 other events, 2959.8 us)
